TPU v7x, 512 devices: a 8x2x16 block of a 8x8x16 slice. The times are simulated.
512 devices in a mesh: groups: 2 (over y), expert: 32 (over z, core), tensor: 8 (over x).
Axes of the slice: x: 8, y: 2, z: 16, core: 2. Of those that a mesh axis runs over, the one named last changes fastest.
The devices are a block of a 8x8x16 slice.
Arguments:
- kv_prefill: bfloat16 [256, 512, 2, 1024], P('groups', 'expert', None, 'tensor'), parts along dimension 0, may hold values from -8 to 8
- slot_of: int32 [256], P('groups'), parts along dimension 0, may hold values from 0 to 127, as said below
- lengths: int32 [256], P('groups'), parts along dimension 0, may hold values from 2 to 512
- query: bfloat16 [256, 4096], P(('groups', 'expert'), 'tensor'), parts along dimension 0, may hold values from -100 to 100
- new_kv: bfloat16 [256, 2, 1024], P(('groups', 'expert'), None, 'tensor'), parts along dimension 0, may hold values from -6 to 6
- wo: bfloat16 [4096, 4096], P('tensor', 'expert'), may hold values from -0.09375 to 0.09375
- resid: bfloat16 [256, 4096], P('groups', 'expert'), parts along dimension 0, may hold values from -60 to 60
- norm_gain: bfloat16 [4096], P('expert'), may hold values from 0.25 to 1.75
- expert_ids: int32 [256, 2], P('groups'), parts along dimension 0, may hold values from 0 to 3, all different within a row; in each aligned block of 128 rows (0 to 127, 128 to 255, ...) at most 96 rows name the same one
- gate_logits: float32 [256, 2], P('groups'), parts along dimension 0, may hold values from -6 to 6
- gate_weight_slabs: bfloat16 [32, 4096, 1024], P('expert', None, 'tensor'), may hold values from -0.09375 to 0.09375
- w_up: bfloat16 [32, 4096, 1024], P('expert', None, 'tensor'), may hold values from -0.09375 to 0.09375
- w_down: bfloat16 [32, 1024, 4096], P('expert', 'tensor'), may hold values from -0.0625 to 0.0625
Outputs:
- attn_out: bfloat16 [256, 4096], P('groups', 'expert'), parts along dimension 0
- moe_out: bfloat16 [256, 4096], P(('groups', 'tensor'), 'expert'), parts along dimension 0
There are 2 independent parts, one for each index of `groups`. A program takes and returns all parts, laid end to end along the dimension named above; an argument that names none is the same for every part. Nothing has to cross between parts.
Inputs may be any that keep to these rules, and one draw needn't show every extreme that they name: `slot_of`: a permutation of 0 to 127. `expert_ids`: each expert is named by at most 96 tokens, one of them by exactly 96; no token names an expert twice.
All inputs are finite; a program needn't handle non-finite values.
Results may differ from a plain program's by a relative error of at most 0.023.
Values may be sent and summed in bfloat16 or wider, within the bound.
A program may use at most 64 MiB of HBM per device.

v0:
```python
import math

import jax
import jax.numpy as jnp
from jax import lax
from jax.sharding import PartitionSpec as P

D = 4096
HEADS = 32
KVH = 8
HD = 128
EXPERTS = 4


EPSILON = 1e-05
MASKED = -1e30


def copy_for_each(array, axis):
    copies = jnp.broadcast_to(array, (lax.axis_size(axis), *array.shape))
    return lax.all_to_all(copies, axis, split_axis=0, concat_axis=0, tiled=True)


def in_order(pieces, dim):
    dims = list(pieces.shape[1:])
    dims[dim] *= pieces.shape[0]
    return jnp.moveaxis(pieces, 0, dim).reshape(dims)


def collect(array, axis, dim):
    pieces = copy_for_each(array, axis)
    return in_order(pieces, dim)


def of_everyone(array, axis):
    return copy_for_each(array, axis).astype(jnp.float32).sum(axis=0)


def taken_together(array, axis):
    return copy_for_each(array, axis).sum(axis=0)


def cut_along(array, dim, size):
    before, after = (array.shape[:dim], array.shape[dim + 1 :])
    return jnp.moveaxis(array.reshape(*before, size, -1, *after), dim, 0)


def summed_on_arrival(array, axis, dim):
    size = lax.axis_size(axis)
    pieces = lax.all_to_all(cut_along(array, dim, size), axis, 0, 0, tiled=True)
    return jnp.sum(pieces.astype(jnp.float32), axis=0)


def cache_partial(query_vectors, key_rows, value_rows, live_mask, logit_scale_factor):
    scores = (
        jnp.einsum("rkqd,rpkd->rkqp", query_vectors, key_rows, preferred_element_type=jnp.float32)
        * logit_scale_factor
    )
    mask_rows = live_mask[:, None, None, :]
    scores = jnp.where(mask_rows, scores, MASKED)
    peak_value = jnp.max(scores, axis=-1)
    exp_weights = jnp.where(mask_rows, jnp.exp(scores - peak_value[..., None]), 0.0)
    denominator = jnp.sum(exp_weights, axis=-1)
    summed = jnp.einsum(
        "rkqp,rpkd->rkqd",
        exp_weights.astype(jnp.bfloat16),
        value_rows,
        preferred_element_type=jnp.float32,
    )
    return (peak_value, denominator, summed)


def combine(earlier, latter):
    peak_value = jnp.maximum(earlier[0], latter[0])
    weight_left = jnp.exp(earlier[0] - peak_value)
    weight_right = jnp.exp(latter[0] - peak_value)
    denominator = earlier[1] * weight_left + latter[1] * weight_right
    summed = earlier[2] * weight_left[..., None] + latter[2] * weight_right[..., None]
    return (peak_value, denominator, summed)


def finish(state, query_vectors, new_rows, logit_scale_factor):
    row_count, kv_local, group_size, head_size = query_vectors.shape
    fresh_key_rows = new_rows[:, 0, :].reshape(row_count, kv_local, head_size)
    new_values = new_rows[:, 1, :].reshape(row_count, kv_local, 1, head_size).astype(jnp.float32)
    self_score_value = (
        jnp.einsum(
            "rkqd,rkd->rkq", query_vectors, fresh_key_rows, preferred_element_type=jnp.float32
        )
        * logit_scale_factor
    )
    own_state = (
        self_score_value,
        jnp.ones_like(self_score_value),
        jnp.broadcast_to(new_values, query_vectors.shape),
    )
    peak_value, denominator, summed = combine(state, own_state)
    return (
        (summed / denominator[..., None])
        .reshape(row_count, kv_local * group_size * head_size)
        .astype(jnp.bfloat16)
    )


def shards(
    kv_prefill,
    slot_of,
    lengths,
    query,
    new_kv,
    wo,
    resid,
    norm_gain,
    expert_ids,
    gate_logits,
    gate_weight_slabs,
    w_up,
    w_down,
):
    axis_count = lax.axis_size("expert")
    my_index = lax.axis_index("expert")
    kv_local = kv_prefill.shape[3] // HD
    group_size = HEADS // KVH
    logit_scale_factor = 1.0 / math.sqrt(HD)
    seq_count = query.shape[0]
    total_rows = lengths.shape[0]
    ordered = jnp.take(kv_prefill, slot_of, axis=0)
    own_cache = lax.all_to_all(ordered, "expert", split_axis=0, concat_axis=1, tiled=True)
    positions = own_cache.shape[1]
    key_rows = own_cache[:, :, 0, :].reshape(seq_count, positions, kv_local, HD)
    value_rows = own_cache[:, :, 1, :].reshape(seq_count, positions, kv_local, HD)
    own_lengths = lax.dynamic_slice_in_dim(lengths, my_index * seq_count, seq_count)
    live_mask = jnp.arange(positions, dtype=jnp.int32)[None, :] < own_lengths[:, None]
    query_vectors = query.reshape(seq_count, kv_local, group_size, HD)
    state = cache_partial(query_vectors, key_rows, value_rows, live_mask, logit_scale_factor)
    context = finish(state, query_vectors, new_kv, logit_scale_factor)
    partial_out = jnp.dot(collect(context, "expert", 0), wo, preferred_element_type=jnp.float32)
    attention = of_everyone(partial_out.astype(jnp.bfloat16), "tensor").astype(jnp.float32)
    attn_out = attention.astype(jnp.bfloat16)
    hidden_activation = resid.astype(jnp.float32) + attn_out.astype(jnp.float32)
    squares = taken_together(jnp.sum(hidden_activation * hidden_activation, axis=1), "expert")
    normed = (
        hidden_activation
        * lax.rsqrt(squares / D + EPSILON)[:, None]
        * norm_gain.astype(jnp.float32)[None, :]
    ).astype(jnp.bfloat16)
    first_share = 1.0 / (1.0 + jnp.exp(gate_logits[:, 1] - gate_logits[:, 0]))
    shares = jnp.stack([first_share, 1.0 - first_share], axis=1)
    sharing = axis_count // EXPERTS
    my_expert = my_index // sharing
    mine_mask = expert_ids == my_expert
    mix_mine = jnp.sum(jnp.where(mine_mask, shares, 0.0), axis=1)
    gate_slab = gate_weight_slabs[0]
    up_slab = w_up[0]
    down_slab = w_down[0]
    capacity = 3 * total_rows // 4
    expert_range = jnp.arange(EXPERTS, dtype=jnp.int32)
    picked = jnp.any(expert_ids[:, :, None] == expert_range[None, None, :], axis=1).astype(
        jnp.int32
    )
    rank_of = jnp.cumsum(picked, axis=0) - 1
    slot_range = jnp.arange(capacity, dtype=jnp.int32)
    slot_hits = (picked[:, :, None] > 0) & (rank_of[:, :, None] == slot_range[None, None, :])
    token_range = jnp.arange(total_rows, dtype=jnp.int32)[:, None, None]
    token_table = jnp.sum(jnp.where(slot_hits, token_range, 0), axis=0)
    token_table = token_table + jnp.where(jnp.any(slot_hits, axis=0), 0, total_rows)
    padded_rows = jnp.concatenate([normed, jnp.zeros((1, normed.shape[1]), jnp.bfloat16)], axis=0)
    blocks = jnp.take(padded_rows, token_table, axis=0)
    outgoing = jnp.repeat(blocks, sharing, axis=0)
    arrived = lax.all_to_all(outgoing, "expert", split_axis=0, concat_axis=2, tiled=True)[0]
    gate_sum = jnp.dot(arrived, gate_slab, preferred_element_type=jnp.float32)
    up_sum = jnp.dot(arrived, up_slab, preferred_element_type=jnp.float32)
    activated = (jax.nn.silu(gate_sum) * up_sum).astype(jnp.bfloat16)
    produced = jnp.dot(activated, down_slab, preferred_element_type=jnp.float32)
    own_picked = jnp.any(mine_mask, axis=1)
    own_rank = jnp.sum(jnp.where(expert_range[None, :] == my_expert, rank_of, 0), axis=1)
    slot_index = jnp.where(own_picked, own_rank, capacity)
    padded_out = jnp.concatenate([produced, jnp.zeros((1, produced.shape[1]), jnp.float32)], axis=0)
    contrib = jnp.take(padded_out, slot_index, axis=0) * mix_mine[:, None]
    token_part = summed_on_arrival(contrib.astype(jnp.bfloat16), "tensor", 0)
    summed_out = summed_on_arrival(token_part.astype(jnp.bfloat16), "expert", 1)
    moe_out = summed_out.astype(jnp.bfloat16)
    return (attn_out, moe_out)


def solution(mesh):
    return jax.shard_map(
        shards,
        mesh=mesh,
        in_specs=(
            P("groups", "expert", None, "tensor"),
            P("groups"),
            P("groups"),
            P(("groups", "expert"), "tensor"),
            P(("groups", "expert"), None, "tensor"),
            P("tensor", "expert"),
            P("groups", "expert"),
            P("expert"),
            P("groups", None),
            P("groups", None),
            P("expert", None, "tensor"),
            P("expert", None, "tensor"),
            P("expert", "tensor", None),
        ),
        out_specs=(P("groups", "expert"), P(("groups", "tensor"), "expert")),
        check_vma=False,
    )
```

profile of v0, /device:TPU:65, one launch (start us, length us, event | category | flops | bytes accessed | tf_op | source)
XLA Modules:
  0.0 281.8 jit_solution(8181250696541056070)
XLA Ops:
  0.6 0.0 copy-start
  0.6 0.7 compare_select_fusion.4
  1.4 0.7 compare_and_fusion.2
  2.1 0.0 copy-done
  2.1 2.7 gather_fusion
  4.7 0.0 copy-start.5
  4.8 0.0 copy-start.8
  4.8 0.0 copy-start.4
  4.8 0.0 copy-start.6
  4.8 2.0 broadcast_select_fusion
  6.8 45.2 %all-to-all-start = ((bf16[128,16,2,128]{3,2,1,0:T(2,128)(2,1)}), bf16[128,16,2,128]{3,2,1,0:T(2,128)(2,1)S(1)}, u32[]{:S(2)}, u32[]{:S(2)}) async-start(bf16[128,16,2,128]{3,2,1,0:T(2,128)(2,1)} %broadcast_select_fusion), calls=%async_computation | async-start | bytes 2097152 | tf_op jit(solution)/shard_map/all_to_all | solution.py:128
  52.1 0.0 copy-done.5
  52.1 0.0 copy-done.8
  52.1 0.1 dynamic_slice.3
  52.2 0.0 copy-done.4
  52.2 0.1 iota_compare_fusion.1
  52.3 0.0 copy-done.6
  52.3 0.1 fusion.36
  52.4 55.3 %all-to-all-done = bf16[128,16,2,128]{3,2,1,0:T(2,128)(2,1)S(1)} async-done(((bf16[128,16,2,128]{3,2,1,0:T(2,128)(2,1)}), bf16[128,16,2,128]{3,2,1,0:T(2,128)(2,1)S(1)}, u32[]{:S(2)}, u32[]{:S(2)}) %all-to-all-start) | async-done | bytes 1048608 | tf_op jit(solution)/shard_map/all_to_all | solution.py:128
  107.7 0.1 copy.33
  107.8 0.0 copy-start.9
  107.9 0.0 copy-start.2
  107.9 0.3 fusion.44
  108.2 0.2 fusion.27
  108.4 0.2 fusion.7
  108.6 0.7 broadcast_in_dim.140
  109.3 4.9 %all-to-all-start.1 = ((bf16[32,4,512]{2,1,0:T(4,128)(2,1)}), bf16[32,4,512]{2,1,0:T(4,128)(2,1)S(1)}, u32[]{:S(2)}, u32[]{:S(2)}) async-start(bf16[32,4,512]{2,1,0:T(4,128)(2,1)} %broadcast_in_dim.140), calls=%async_computation.1 | async-start | bytes 262144 | tf_op jit(solution)/shard_map/all_to_all | solution.py:21
  114.2 0.1 copy.34
  114.3 0.2 reduce_window_sum.11
  114.5 0.1 select_reduce_fusion.1
  114.6 0.1 copy.36
  114.7 0.2 select_reduce_fusion
  114.9 15.2 %all-to-all-done.1 = bf16[32,4,512]{2,1,0:T(4,128)(2,1)S(1)} async-done(((bf16[32,4,512]{2,1,0:T(4,128)(2,1)}), bf16[32,4,512]{2,1,0:T(4,128)(2,1)S(1)}, u32[]{:S(2)}, u32[]{:S(2)}) %all-to-all-start.1) | async-done | bytes 131104 | tf_op jit(solution)/shard_map/all_to_all | solution.py:21
  130.2 0.2 convolution_convert_fusion
  130.3 0.7 broadcast_in_dim.141
  131.1 6.2 %all-to-all-start.2 = ((bf16[8,128,128]{2,1,0:T(8,128)(2,1)}), bf16[8,128,128]{2,1,0:T(8,128)(2,1)S(1)}, u32[]{:S(2)}, u32[]{:S(2)}) async-start(bf16[8,128,128]{2,1,0:T(8,128)(2,1)} %broadcast_in_dim.141), calls=%async_computation.2 | async-start | bytes 524288 | tf_op jit(solution)/shard_map/all_to_all | solution.py:21
  137.3 0.1 fusion.20
  137.5 0.0 copy-done.9
  137.5 0.1 reshape.234
  137.6 9.4 %all-to-all-done.2 = bf16[8,128,128]{2,1,0:T(8,128)(2,1)S(1)} async-done(((bf16[8,128,128]{2,1,0:T(8,128)(2,1)}), bf16[8,128,128]{2,1,0:T(8,128)(2,1)S(1)}, u32[]{:S(2)}, u32[]{:S(2)}) %all-to-all-start.2) | async-done | bytes 262176 | tf_op jit(solution)/shard_map/all_to_all | solution.py:21
  147.1 0.0 copy-start.1
  147.1 0.1 multiply_reduce_fusion
  147.2 0.6 broadcast_in_dim.152
  147.8 6.9 %all-to-all-start.3 = ((f32[32,1,128]{2,1,0:T(1,128)}), f32[32,1,128]{2,1,0:T(1,128)S(1)}, u32[]{:S(2)}, u32[]{:S(2)}) async-start(f32[32,1,128]{2,1,0:T(1,128)} %broadcast_in_dim.152), calls=%async_computation.3 | async-start | bytes 32768 | tf_op jit(solution)/shard_map/all_to_all | solution.py:21
  154.7 11.9 %all-to-all-done.3 = f32[32,1,128]{2,1,0:T(1,128)S(1)} async-done(((f32[32,1,128]{2,1,0:T(1,128)}), f32[32,1,128]{2,1,0:T(1,128)S(1)}, u32[]{:S(2)}, u32[]{:S(2)}) %all-to-all-start.3) | async-done | bytes 16416 | tf_op jit(solution)/shard_map/all_to_all | solution.py:21
  166.6 0.1 multiply_convert_fusion.1
  166.7 1.4 gather_fusion.1
  168.1 0.1 broadcast_select_fusion.1
  168.3 1.0 broadcast_in_dim.155
  169.3 4.7 %all-to-all-start.4 = ((bf16[32,96,128]{2,1,0:T(8,128)(2,1)}), bf16[32,96,128]{2,1,0:T(8,128)(2,1)S(1)}, u32[]{:S(2)}, u32[]{:S(2)}) async-start(bf16[32,96,128]{2,1,0:T(8,128)(2,1)} %bitcast.14), calls=%async_computation.4 | async-start | bytes 1572864 | tf_op jit(solution)/shard_map/all_to_all | solution.py:170
  174.0 0.1 select_n.125
  174.1 0.1 mul.90
  174.2 44.2 %all-to-all-done.4 = bf16[32,96,128]{2,1,0:T(8,128)(2,1)S(1)} async-done(((bf16[32,96,128]{2,1,0:T(8,128)(2,1)}), bf16[32,96,128]{2,1,0:T(8,128)(2,1)S(1)}, u32[]{:S(2)}, u32[]{:S(2)}) %all-to-all-start.4) | async-done | bytes 786464 | tf_op jit(solution)/shard_map/all_to_all | solution.py:170
  218.5 0.3 copy.38
  218.8 1.7 fusion.11
  220.5 3.5 %fusion.3 = f32[96,4096]{1,0:T(8,128)} fusion(bf16[1,128,4096]{2,1,0:T(8,128)(2,1)} %param.25, bf16[1,4096,128]{2,1,0:T(8,128)(2,1)} %param.24, bf16[12,8,32,128]{3,2,1,0:T(8,128)(2,1)S(1)} %bitcast.68, f32[96,128]{1,0:T(8,128)S(1)} %fusion.11), kind=kOutput, calls=%fused_computation.11 | convolution fusion | flops 201400320 | bytes 4505600 | tf_op jit(solution)/shard_map/dot_general | solution.py:174
  224.0 1.6 concatenate.7
  225.5 2.6 gather_fusion.2
  228.1 1.9 multiply_convert_fusion
  230.0 29.9 %all_to_all.59 = bf16[8,16,4096]{2,1,0:T(8,128)(2,1)S(1)} all-to-all(bf16[8,16,4096]{2,1,0:T(8,128)(2,1)S(1)} %multiply_convert_fusion), channel_id=1, replica_groups=mesh['groups'=2,'expert'=32,'tensor'=8] {'tensor'}, dimensions={0} | all-to-all | bytes 2097152 | tf_op jit(solution)/shard_map/all_to_all | solution.py:50
  259.9 0.1 reduce_sum.97
  260.1 0.1 copy.39
  260.2 21.0 %all_to_all.60 = bf16[32,16,128]{2,1,0:T(8,128)(2,1)S(1)} all-to-all(bf16[32,16,128]{2,1,0:T(8,128)(2,1)S(1)} %copy.39), channel_id=1, replica_groups=mesh['groups'=2,'expert'=32,'tensor'=8] {'expert'}, dimensions={0} | all-to-all | bytes 262144 | tf_op jit(solution)/shard_map/all_to_all | solution.py:50
  281.1 0.6 reduce_sum.98
  (30 shorter events, 0.3 us)
Async XLA Ops:
  0.6 1.4 copy-start
  4.7 47.4 %copy-start.5 = (bf16[4,512]{1,0:T(4,128)(2,1)S(1)}, bf16[4,512]{1,0:T(4,128)(2,1)}, u32[]{:S(2)}) copy-start(bf16[4,512]{1,0:T(4,128)(2,1)} %param.16) | copy-start | bytes 12292
  4.8 47.4 %copy-start.8 = (s32[128]{0:T(128)S(1)}, s32[128]{0:T(128)}, u32[]{:S(2)}) copy-start(s32[128]{0:T(128)} %param.15) | copy-start | bytes 1540
  4.8 47.4 %copy-start.4 = (s32[128,2]{0,1:T(2,128)S(1)}, s32[128,2]{0,1:T(2,128)}, u32[]{:S(2)}) copy-start(s32[128,2]{0,1:T(2,128)} %param.21) | copy-start | bytes 3076
  4.8 47.5 %copy-start.6 = (bf16[4,2,128]{2,1,0:T(2,128)(2,1)S(1)}, bf16[4,2,128]{2,1,0:T(2,128)(2,1)}, u32[]{:S(2)}) copy-start(bf16[4,2,128]{2,1,0:T(2,128)(2,1)} %param.17) | copy-start | bytes 6148
  6.8 100.9 %all-to-all-start = ((bf16[128,16,2,128]{3,2,1,0:T(2,128)(2,1)}), bf16[128,16,2,128]{3,2,1,0:T(2,128)(2,1)S(1)}, u32[]{:S(2)}, u32[]{:S(2)}) async-start(bf16[128,16,2,128]{3,2,1,0:T(2,128)(2,1)} %broadcast_select_fusion), calls=%async_computation | async-start | bytes 2097152 | tf_op jit(solution)/shard_map/all_to_all | solution.py:128
  107.7 22.5 %copy-start.3 = (bf16[512,128]{1,0:T(8,128)(2,1)S(1)}, bf16[512,128]{1,0:T(8,128)(2,1)}, u32[]{:S(2)}) copy-start(bf16[512,128]{1,0:T(8,128)(2,1)} %param.18) | copy-start | bytes 393220
  107.8 29.6 %copy-start.9 = (bf16[128]{0:T(256)(128)(2,1)S(1)}, bf16[128]{0:T(256)(128)(2,1)}, u32[]{:S(2)}) copy-start(bf16[128]{0:T(256)(128)(2,1)} %param.20) | copy-start | bytes 772
  107.9 39.2 %copy-start.2 = (bf16[128,128]{1,0:T(8,128)(2,1)S(1)}, bf16[128,128]{1,0:T(8,128)(2,1)}, u32[]{:S(2)}) copy-start(bf16[128,128]{1,0:T(8,128)(2,1)} %param.19) | copy-start | bytes 98308
  109.3 20.8 %all-to-all-start.1 = ((bf16[32,4,512]{2,1,0:T(4,128)(2,1)}), bf16[32,4,512]{2,1,0:T(4,128)(2,1)S(1)}, u32[]{:S(2)}, u32[]{:S(2)}) async-start(bf16[32,4,512]{2,1,0:T(4,128)(2,1)} %broadcast_in_dim.140), calls=%async_computation.1 | async-start | bytes 262144 | tf_op jit(solution)/shard_map/all_to_all | solution.py:21
  131.1 15.9 %all-to-all-start.2 = ((bf16[8,128,128]{2,1,0:T(8,128)(2,1)}), bf16[8,128,128]{2,1,0:T(8,128)(2,1)S(1)}, u32[]{:S(2)}, u32[]{:S(2)}) async-start(bf16[8,128,128]{2,1,0:T(8,128)(2,1)} %broadcast_in_dim.141), calls=%async_computation.2 | async-start | bytes 524288 | tf_op jit(solution)/shard_map/all_to_all | solution.py:21
  137.3 36.8 %copy-start.7 = (f32[128,2]{0,1:T(2,128)S(1)}, f32[128,2]{0,1:T(2,128)}, u32[]{:S(2)}) copy-start(f32[128,2]{0,1:T(2,128)} %param.22) | copy-start | bytes 3076
  147.1 71.7 %copy-start.1 = (bf16[128,128]{1,0:T(8,128)(2,1)}, bf16[128,128]{1,0:T(8,128)(2,1)S(1)}, u32[]{:S(2)}) copy-start(bf16[128,128]{1,0:T(8,128)(2,1)S(1)} %reduce_sum.91) | copy-start | bytes 98308
  147.8 18.7 %all-to-all-start.3 = ((f32[32,1,128]{2,1,0:T(1,128)}), f32[32,1,128]{2,1,0:T(1,128)S(1)}, u32[]{:S(2)}, u32[]{:S(2)}) async-start(f32[32,1,128]{2,1,0:T(1,128)} %broadcast_in_dim.152), calls=%async_computation.3 | async-start | bytes 32768 | tf_op jit(solution)/shard_map/all_to_all | solution.py:21
  169.3 49.2 %all-to-all-start.4 = ((bf16[32,96,128]{2,1,0:T(8,128)(2,1)}), bf16[32,96,128]{2,1,0:T(8,128)(2,1)S(1)}, u32[]{:S(2)}, u32[]{:S(2)}) async-start(bf16[32,96,128]{2,1,0:T(8,128)(2,1)} %bitcast.14), calls=%async_computation.4 | async-start | bytes 1572864 | tf_op jit(solution)/shard_map/all_to_all | solution.py:170
where the time goes:
time: 283 us; the launch traced here: 282 us
  waiting for transfers between devices  136 us (48%)
  starting transfers between devices  67.9 us (24%)
  blocking collectives  50.9 us (18%)
  local copies, waits for them, and re-layouts  12.4 us (4%)
  other arithmetic  7.48 us (3%)
  matrix products  6.03 us (2%)
    all_to_all x1, waiting for transfers between devices, shards(): lax.all_to_all(ordered, 'expert', split_axis=0, concat_axis=1, tiled=True)  55.3 us
    all_to_all x2, blocking collectives, summed_on_arrival(): pieces = lax.all_to_all(cut_along(array, dim, size), axis, 0, 0, tiled=True)  50.9 us
    all_to_all x1, starting transfers between devices, shards(): lax.all_to_all(ordered, 'expert', split_axis=0, concat_axis=1, tiled=True)  45.2 us
    all_to_all x1, waiting for transfers between devices, shards(): lax.all_to_all(outgoing, 'expert', split_axis=0, concat_axis=2, tiled=True)  44.2 us
    all_to_all x3, waiting for transfers between devices, copy_for_each(): return lax.all_to_all(copies, axis, split_axis=0, concat_axis=0, tiled=True)  36.5 us
    all_to_all x3, starting transfers between devices, copy_for_each(): return lax.all_to_all(copies, axis, split_axis=0, concat_axis=0, tiled=True)  18 us
  transfers between devices with their start and end apart: 5, of which 5 were waited for; matrix products, arithmetic and copies ran while one was open for 1% of the time, Pallas kernels for 0%

commit v1 on v0

v1 whole, which is shorter than its diff:
```python
import functools
import math

import jax
import jax.numpy as jnp
from jax import lax
from jax.experimental import pallas as pl
from jax.experimental.pallas import tpu as pltpu
from jax.sharding import PartitionSpec as P

HD = 128
EXPERTS = 4
EPSILON = 1e-05
MASKED = -1e30
MESH = pl.DeviceIdType.MESH
F32 = jnp.float32
BF16 = jnp.bfloat16


def around(step, n):
    half = n // 2
    return half + ((step + 1) // 2) * (1 - 2 * (step % 2))


def kernel(
    ne,
    nt,
    slot_ref,
    lens_ref,
    ids_ref,
    logits_ref,
    q_ref,
    nk_ref,
    resid_ref,
    gain_ref,
    kv_hbm,
    wo_hbm,
    wg_hbm,
    wu_hbm,
    wd_hbm,
    attn_ref,
    moe_ref,
    kv,
    wo,
    wgu,
    wd,
    qf,
    q_all,
    osend,
    orecv,
    lsend,
    lrecv,
    ctx_all,
    cf,
    psend,
    precv,
    attn_all,
    hsend,
    ssend,
    srecv,
    ssx,
    xbuf,
    act,
    ysend,
    yrecv,
    zsend,
    zrecv,
    load_sem,
    wd_sem,
    q_sem,
    o_sem,
    l_sem,
    c_sem,
    p_sem,
    t_sem,
    a_send,
    a_recv,
    s_sem,
    ssx_sem,
    b_send,
    b_recv,
    f_send,
    f_recv,
    act_sem,
    y_send,
    y_recv,
    z_sem,
):
    i = lax.axis_index("expert")
    x = lax.axis_index("tensor")
    nz = ne // 2
    z = i // 2
    c = i % 2
    partner = i + 1 - 2 * c
    scale = 1.0 / math.sqrt(HD)
    tokens = lens_ref.shape[1]
    heads = q_ref.shape[1] // HD
    seqs = q_ref.shape[0]
    rows = seqs * heads
    block = tokens // nt
    width = gain_ref.shape[1]

    def remote(src, dst, send, recv, **where):
        return pltpu.make_async_remote_copy(
            src_ref=src,
            dst_ref=dst,
            send_sem=send,
            recv_sem=recv,
            device_id=where,
            device_id_type=MESH,
        )

    def loop(count, body):
        def step(s, carry):
            body(s)
            return carry

        lax.fori_loop(0, count, step, 0)

    kv_load = pltpu.make_async_copy(kv_hbm, kv, load_sem.at[0])
    wo_load = pltpu.make_async_copy(wo_hbm, wo, load_sem.at[1])
    wg_load = pltpu.make_async_copy(wg_hbm, wgu.at[:, pl.ds(0, HD)], load_sem.at[2])
    wu_load = pltpu.make_async_copy(wu_hbm, wgu.at[:, pl.ds(HD, HD)], load_sem.at[3])
    kv_load.start()
    wo_load.start()
    wg_load.start()
    wu_load.start()
    own_rows = pl.ds(pl.multiple_of(c * HD, HD), HD)

    def load_down(s):
        col = pl.multiple_of((2 * s + c) * HD, HD)
        pltpu.make_async_copy(
            wd_hbm.at[:, pl.ds(col, HD)],
            wd.at[own_rows, pl.ds(pl.multiple_of(s * HD, HD), HD)],
            load_sem.at[4],
        ).start()

    loop(nz, load_down)

    barrier = pltpu.get_barrier_semaphore()

    def greet_expert(s):
        j = (i + around(s, ne)) % ne
        pl.semaphore_signal(barrier, inc=1, device_id={"expert": j}, device_id_type=MESH)

    def greet_tensor(s):
        j = (x + around(s, nt)) % nt
        pl.semaphore_signal(barrier, inc=1, device_id={"tensor": j}, device_id_type=MESH)

    loop(ne - 1, greet_expert)
    loop(nt - 1, greet_tensor)

    for h in range(heads):
        qf[pl.ds(h, seqs, stride=heads), :] = q_ref[:, h * HD : (h + 1) * HD].astype(F32)
    q_own = qf[...]
    q_all[i] = q_own.astype(BF16)
    row16 = lax.broadcasted_iota(jnp.int32, (rows, HD), 0)
    key_rows = jnp.zeros((rows, HD), F32)
    value_rows = jnp.zeros((rows, HD), F32)
    for b in range(seqs):
        mine = (row16 // heads) == b
        pair = nk_ref[b].astype(F32)
        key_rows = jnp.where(mine, pair[0:1, :], key_rows)
        value_rows = jnp.where(mine, pair[1:2, :], value_rows)
    own_score = jnp.sum(q_own * key_rows, axis=1, keepdims=True) * scale

    pl.semaphore_wait(barrier, ne - 1 + nt - 1)

    def send_q(s):
        j = (i + around(s, ne)) % ne
        remote(q_all.at[i], q_all.at[i], q_sem.at[0], q_sem.at[1], expert=j).start()

    loop(ne - 1, send_q)

    def send_down(s):
        col = pl.multiple_of((2 * s + 1 - c) * HD, HD)
        remote(
            wd_hbm.at[:, pl.ds(col, HD)],
            wd.at[own_rows, pl.ds(pl.multiple_of(s * HD, HD), HD)],
            wd_sem.at[0],
            wd_sem.at[1],
            expert=partner,
        ).start()

    loop(nz, send_down)

    kv_load.wait()
    remote(
        q_all.at[pl.ds(0, ne - 1)], q_all.at[pl.ds(0, ne - 1)], q_sem.at[0], q_sem.at[1], expert=partner
    ).wait_recv()
    per = 4
    groups = ne // per
    grows = per * rows
    span = kv.shape[1]
    gcols = per * seqs * span
    row_of = lax.broadcasted_iota(jnp.int32, (grows, gcols), 0) // heads
    rel = lax.broadcasted_iota(jnp.int32, (grows, gcols), 1) - row_of * span
    rel = jnp.where((rel >= 0) & (rel < span) & (rel % 2 == 0), rel, 1 << 20)
    lane = lax.broadcasted_iota(jnp.int32, (grows, HD), 1)
    grow = lax.broadcasted_iota(jnp.int32, (grows, HD), 0)
    lens = lens_ref[...].astype(F32)

    def attend(s):
        g = (i // per + around(s, groups)) % groups
        kvb = jnp.concatenate(
            [kv[slot_ref[g * per * seqs + t]] for t in range(per * seqs)], axis=0
        )
        qg = q_all[pl.ds(g * per, per)].reshape(grows, HD)
        scores = (
            lax.dot_general(qg, kvb, (((1,), (1,)), ((), ())), preferred_element_type=F32) * scale
        )
        hit = lane == g * per * seqs + grow // heads
        length = jnp.sum(jnp.where(hit, lens, 0.0), axis=1, keepdims=True)
        live = (2.0 * length).astype(jnp.int32) - i * span
        valid = rel < live
        scores = jnp.where(valid, scores, MASKED)
        peak = jnp.max(scores, axis=1, keepdims=True)
        weights = jnp.where(valid, jnp.exp(scores - peak), 0.0)
        total = jnp.sum(weights, axis=1, keepdims=True)
        shifted = pltpu.roll(weights, 1, axis=1).astype(BF16)
        summed = jnp.dot(shifted, kvb, preferred_element_type=F32)
        some = total > 0.0
        safe = jnp.where(some, total, 1.0)
        osend[pl.ds(g * per, per)] = (summed / safe).astype(BF16).reshape(per, rows, HD)
        lse = jnp.where(some, peak + jnp.log(safe), MASKED)
        spread = jnp.where(lane == grow % rows, lse, 0.0).reshape(per, rows, HD)
        lsend[pl.ds(g * per, per)] = jnp.sum(spread, axis=1, keepdims=True)
        for t in range(per):
            j = g * per + t

            @pl.when(j != i)
            def _():
                remote(osend.at[j], orecv.at[i], o_sem.at[0], o_sem.at[1], expert=j).start()
                remote(lsend.at[j], lrecv.at[i], l_sem.at[0], l_sem.at[1], expert=j).start()

            @pl.when(j == i)
            def _():
                orecv[i] = osend[j]
                lrecv[i] = lsend[j]

    loop(groups, attend)

    some_blocks = pl.ds(0, ne - 1)
    o_all = remote(
        osend.at[some_blocks], orecv.at[some_blocks], o_sem.at[0], o_sem.at[1], expert=partner
    )
    l_all = remote(
        lsend.at[some_blocks], lrecv.at[some_blocks], l_sem.at[0], l_sem.at[1], expert=partner
    )
    l_all.wait_recv()
    o_all.wait_recv()
    lses = lrecv[...].reshape(ne, HD)
    lses = jnp.concatenate([lses, jnp.zeros((HD - ne, HD), F32)], axis=0).T[:rows, :ne]
    top = jnp.maximum(jnp.max(lses, axis=1, keepdims=True), own_score)
    parts = jnp.exp(lses - top)
    own_part = jnp.exp(own_score - top)
    inverse = 1.0 / (jnp.sum(parts, axis=1, keepdims=True) + own_part)
    parts = parts * inverse
    context = own_part * inverse * value_rows
    for j in range(ne):
        context = context + parts[:, j : j + 1] * orecv[j].astype(F32)
    ctx_all[i] = context.astype(BF16)

    def send_ctx(s):
        j = (i + around(s, ne)) % ne
        remote(ctx_all.at[i], ctx_all.at[i], c_sem.at[0], c_sem.at[1], expert=j).start()

    loop(ne - 1, send_ctx)
    wo_load.wait()
    c_all = remote(
        ctx_all.at[some_blocks], ctx_all.at[some_blocks], c_sem.at[0], c_sem.at[1], expert=partner
    )
    c_all.wait_recv()
    cf[...] = ctx_all[...].reshape(ne * rows, HD).astype(F32)
    partial = jnp.zeros((tokens, width), F32)
    for h in range(heads):
        head_rows = cf[pl.ds(h, tokens, stride=heads), :].astype(BF16)
        partial = partial + jnp.dot(
            head_rows, wo[h * HD : (h + 1) * HD, :], preferred_element_type=F32
        )
    psend[...] = partial.astype(BF16).reshape(nt, block, width)

    def send_p(s):
        j = (x + around(s, nt)) % nt
        remote(psend.at[j], precv.at[x], p_sem.at[0], p_sem.at[1], tensor=j).start()

    loop(nt - 1, send_p)
    precv[x] = psend[x]
    few = pl.ds(0, nt - 1)
    next_x = (x + 1) % nt
    p_all = remote(psend.at[few], precv.at[few], p_sem.at[0], p_sem.at[1], tensor=next_x)
    p_all.wait_recv()
    attn = jnp.sum(precv[...].astype(F32), axis=0).astype(BF16)
    attn_all[x] = attn
    hidden = resid_ref[pl.ds(pl.multiple_of(x * block, block), block), :].astype(F32) + attn.astype(
        F32
    )
    hsend[...] = (hidden * gain_ref[...].astype(F32)).astype(BF16)
    squares = jnp.sum(hidden * hidden, axis=1, keepdims=True)
    lane_b = lax.broadcasted_iota(jnp.int32, (block, HD), 1)
    row_b = lax.broadcasted_iota(jnp.int32, (block, HD), 0)
    ssend[...] = jnp.sum(jnp.where(lane_b == row_b, squares, 0.0), axis=0, keepdims=True)

    half = i // nz
    xbuf_slot = xbuf.at[x, i]

    def send_a(s):
        zz = (z + around(s, nz)) % nz
        j = 2 * zz + half

        @pl.when(j != i)
        def _():
            remote(hsend, xbuf_slot, a_send, a_recv.at[i % nz], expert=j).start()

        @pl.when(j == i)
        def _():
            xbuf[x, i] = hsend[...]

    loop(nz, send_a)

    def send_s(s):
        j = (i + around(s, ne)) % ne
        remote(ssend, srecv.at[i], s_sem.at[0], s_sem.at[1], expert=j).start()

    loop(ne - 1, send_s)
    srecv[i] = ssend[...]

    def send_t(s):
        j = (x + around(s, nt)) % nt
        remote(attn_all.at[x], attn_all.at[x], t_sem.at[0], t_sem.at[1], tensor=j).start()

    chunk = 4
    chunks = nz // chunk

    def spread_chunk(k):
        def arrive(t):
            src = c * nz + k * chunk + t

            @pl.when(src != i)
            def _():
                remote(hsend, xbuf.at[x, src], a_send, a_recv.at[src % nz], expert=partner).wait_recv()

        loop(chunk, arrive)
        piece = pl.ds(c * nz + k * chunk, chunk)

        def send_b(s):
            j = (x + around(s, nt)) % nt
            remote(
                xbuf.at[x, piece], xbuf.at[x, piece], b_send, b_recv.at[x, k], tensor=j
            ).start()

        loop(nt - 1, send_b)
        remote(xbuf.at[x, piece], xbuf.at[x, piece], f_send, f_recv.at[x, k], expert=partner).start()

    loop(chunks, spread_chunk)

    s_all = remote(srecv.at[some_blocks], srecv.at[some_blocks], s_sem.at[0], s_sem.at[1], expert=partner)
    s_all.wait_recv()
    ssx[x] = jnp.sum(srecv[...], axis=0)

    def send_ssx(s):
        j = (x + around(s, nt)) % nt
        remote(ssx.at[x], ssx.at[x], ssx_sem.at[0], ssx_sem.at[1], tensor=j).start()

    loop(nt - 1, send_ssx)

    def forward_chunk(k):
        piece = pl.ds(c * nz + k * chunk, chunk)

        def forward(s):
            j = (x + around(nt - 2 - s, nt)) % nt
            hop = remote(
                xbuf.at[j, piece], xbuf.at[j, piece], f_send, f_recv.at[j, k], expert=partner
            )
            remote(
                xbuf.at[j, piece], xbuf.at[j, piece], b_send, b_recv.at[j, k], tensor=next_x
            ).wait_recv()
            hop.start()

        loop(nt - 1, forward)

    loop(chunks, forward_chunk)
    loop(nt - 1, send_t)

    expert = i // (ne // EXPERTS)
    first = 1.0 / (1.0 + jnp.exp(logits_ref[1:2, :] - logits_ref[0:1, :]))
    mixture = jnp.where(ids_ref[0:1, :] == expert, first, 0.0) + jnp.where(
        ids_ref[1:2, :] == expert, 1.0 - first, 0.0
    )
    lane_t = lax.broadcasted_iota(jnp.int32, (tokens, tokens), 1)
    row_t = lax.broadcasted_iota(jnp.int32, (tokens, tokens), 0)
    mixture = jnp.sum(jnp.where(lane_t == row_t, mixture, 0.0), axis=1, keepdims=True)

    ssx_all = remote(ssx.at[few], ssx.at[few], ssx_sem.at[0], ssx_sem.at[1], tensor=next_x)
    ssx_all.wait_recv()
    sums = ssx[...].reshape(nt, HD)
    sums = jnp.concatenate([sums, jnp.zeros((HD - nt, HD), F32)], axis=0).T
    sums = jnp.concatenate([sums[:block, t : t + 1] for t in range(nt)], axis=0)
    factor = lax.rsqrt(sums / (ne * width) + EPSILON)

    wg_load.wait()
    wu_load.wait()

    def arrived_chunk(k):
        piece = pl.ds((1 - c) * nz + k * chunk, chunk)

        def arrived(j):
            remote(
                xbuf.at[j, piece], xbuf.at[j, piece], f_send, f_recv.at[j, k], expert=partner
            ).wait_recv()

        loop(nt, arrived)

    loop(chunks, arrived_chunk)

    def gate_up(k, acc):
        left = jnp.concatenate(
            [xbuf[:, 2 * k + t].reshape(tokens, width) for t in range(2)], axis=1
        )
        right = wgu[pl.ds(pl.multiple_of(2 * k * width, 2 * width), 2 * width), :]
        return acc + jnp.dot(left, right, preferred_element_type=F32)

    both = lax.fori_loop(0, ne // 2, gate_up, jnp.zeros((tokens, 2 * HD), F32))
    gate = both[:, :HD] * factor
    up = both[:, HD:] * factor
    activated = gate / (1.0 + jnp.exp(-gate)) * up * mixture
    act[c] = activated.astype(BF16)
    act_hop = remote(act.at[c], act.at[c], act_sem.at[0], act_sem.at[1], expert=partner)
    act_hop.start()
    remote(
        wd_hbm.at[:, pl.ds(0, nz * HD)],
        wd.at[pl.ds(0, HD), :],
        wd_sem.at[0],
        wd_sem.at[1],
        expert=partner,
    ).wait()
    pltpu.make_async_copy(
        wd_hbm.at[:, pl.ds(0, nz * HD)], wd.at[pl.ds(0, HD), :], load_sem.at[4]
    ).wait()
    act_hop.wait_recv()

    left = jnp.concatenate([act[0], act[1]], axis=1)
    pieces = ysend.shape[0]
    deep = ysend.shape[2]

    def down(k):
        cols = pl.ds(pl.multiple_of(k * deep * width, deep * width), deep * width)
        made = jnp.dot(left, wd[:, cols], preferred_element_type=F32).astype(BF16)
        for t in range(deep):
            ysend[k, :, t] = made[:, t * width : (t + 1) * width].reshape(nt, block, width)

        def send_y(s):
            j = (x + around(s, nt)) % nt
            remote(ysend.at[k, j], yrecv.at[k, x], y_send, y_recv.at[k], tensor=j).start()

        loop(nt - 1, send_y)
        yrecv[k, x] = ysend[k, x]

    loop(pieces, down)

    def fold(k):
        remote(
            ysend.at[k, few], yrecv.at[k, few], y_send, y_recv.at[k], tensor=next_x
        ).wait_recv()
        folded = jnp.sum(yrecv[k].astype(F32), axis=0).astype(BF16)
        zsend[pl.ds(k * deep, deep)] = folded

        def send_z(t):
            zz = k * deep + t

            @pl.when(zz != z)
            def _():
                remote(
                    zsend.at[zz], zrecv.at[z], z_sem.at[0], z_sem.at[1], expert=2 * zz + c
                ).start()

            @pl.when(zz == z)
            def _():
                zrecv[z] = zsend[zz]

        loop(deep, send_z)

    loop(pieces, fold)
    most = pl.ds(0, nz - 1)
    z_all = remote(zsend.at[most], zrecv.at[most], z_sem.at[0], z_sem.at[1], expert=partner)
    z_all.wait_recv()
    moe_ref[...] = jnp.sum(zrecv[...].astype(F32), axis=0).astype(BF16)

    t_all = remote(attn_all.at[few], attn_all.at[few], t_sem.at[0], t_sem.at[1], tensor=next_x)
    t_all.wait_recv()
    attn_ref[...] = attn_all[...].reshape(tokens, width)

    remote(
        q_all.at[some_blocks], q_all.at[some_blocks], q_sem.at[0], q_sem.at[1], expert=partner
    ).wait_send()
    o_all.wait_send()
    l_all.wait_send()
    c_all.wait_send()
    p_all.wait_send()
    s_all.wait_send()
    ssx_all.wait_send()
    t_all.wait_send()
    z_all.wait_send()
    act_hop.wait_send()

    self_fed = jnp.where(half == c, 1, 0)

    @pl.when(self_fed == 1)
    def _():
        remote(xbuf.at[0, most], xbuf.at[0, most], a_send, a_recv.at[0], expert=partner).wait_send()

    @pl.when(self_fed == 0)
    def _():
        all_z = pl.ds(0, nz)
        remote(xbuf.at[0, all_z], xbuf.at[0, all_z], a_send, a_recv.at[0], expert=partner).wait_send()

    mine = pl.ds(0, nz)
    remote(xbuf.at[few, mine], xbuf.at[few, mine], b_send, b_recv.at[0, 0], tensor=next_x).wait_send()
    all_x = pl.ds(0, nt)
    remote(xbuf.at[all_x, mine], xbuf.at[all_x, mine], f_send, f_recv.at[0, 0], expert=partner).wait_send()
    remote(ysend.at[:, few], yrecv.at[:, few], y_send, y_recv.at[0], tensor=next_x).wait_send()


def solution(mesh):
    ne = mesh.shape["expert"]
    nt = mesh.shape["tensor"]
    nz = ne // 2

    def shards(
        kv_prefill,
        slot_of,
        lengths,
        query,
        new_kv,
        wo,
        resid,
        norm_gain,
        expert_ids,
        gate_logits,
        gate_weight_slabs,
        w_up,
        w_down,
    ):
        slots, held = kv_prefill.shape[:2]
        tokens = lengths.shape[0]
        seqs, qcols = query.shape
        heads = qcols // HD
        rows = seqs * heads
        block = tokens // nt
        width = wo.shape[1]
        depth = gate_weight_slabs.shape[1]
        deep = 4
        smem = pl.BlockSpec(memory_space=pltpu.SMEM)
        vmem = pl.BlockSpec(memory_space=pltpu.VMEM)
        anywhere = pl.BlockSpec(memory_space=pl.ANY)
        dma = pltpu.SemaphoreType.DMA
        return pl.pallas_call(
            functools.partial(kernel, ne, nt),
            out_shape=(
                jax.ShapeDtypeStruct((tokens, width), BF16),
                jax.ShapeDtypeStruct((block, width), BF16),
            ),
            in_specs=[smem] + [vmem] * 7 + [anywhere] * 5,
            out_specs=(vmem, vmem),
            scratch_shapes=[
                pltpu.VMEM((slots, 2 * held, HD), BF16),
                pltpu.VMEM(wo.shape, BF16),
                pltpu.VMEM((depth, 2 * HD), BF16),
                pltpu.VMEM((2 * HD, nz * width), BF16),
                pltpu.VMEM((rows, HD), F32),
                pltpu.VMEM((ne, rows, HD), BF16),
                pltpu.VMEM((ne, rows, HD), BF16),
                pltpu.VMEM((ne, rows, HD), BF16),
                pltpu.VMEM((ne, 1, HD), F32),
                pltpu.VMEM((ne, 1, HD), F32),
                pltpu.VMEM((ne, rows, HD), BF16),
                pltpu.VMEM((ne * rows, HD), F32),
                pltpu.VMEM((nt, block, width), BF16),
                pltpu.VMEM((nt, block, width), BF16),
                pltpu.VMEM((nt, block, width), BF16),
                pltpu.VMEM((block, width), BF16),
                pltpu.VMEM((1, HD), F32),
                pltpu.VMEM((ne, 1, HD), F32),
                pltpu.VMEM((nt, 1, HD), F32),
                pltpu.VMEM((nt, ne, block, width), BF16),
                pltpu.VMEM((2, tokens, HD), BF16),
                pltpu.VMEM((nz // deep, nt, deep, block, width), BF16),
                pltpu.VMEM((nz // deep, nt, deep, block, width), BF16),
                pltpu.VMEM((nz, block, width), BF16),
                pltpu.VMEM((nz, block, width), BF16),
                dma((5,)),
                dma((2,)),
                dma((2,)),
                dma((2,)),
                dma((2,)),
                dma((2,)),
                dma((2,)),
                dma((2,)),
                dma,
                dma((nz,)),
                dma((2,)),
                dma((2,)),
                dma,
                dma((nt, nz // 4)),
                dma,
                dma((nt, nz // 4)),
                dma((2,)),
                dma,
                dma((nz // deep,)),
                dma((2,)),
            ],
            compiler_params=pltpu.CompilerParams(
                collective_id=0, has_side_effects=True, vmem_limit_bytes=48 * 1024 * 1024
            ),
        )(
            slot_of,
            lengths.reshape(1, tokens),
            expert_ids.T,
            gate_logits.T,
            query,
            new_kv,
            resid,
            norm_gain.reshape(1, width),
            kv_prefill.reshape(slots, 2 * held, HD),
            wo,
            gate_weight_slabs.reshape(depth, HD),
            w_up.reshape(depth, HD),
            w_down.reshape(HD, ne * width),
        )

    return jax.shard_map(
        shards,
        mesh=mesh,
        in_specs=(
            P("groups", "expert", None, "tensor"),
            P("groups"),
            P("groups"),
            P(("groups", "expert"), "tensor"),
            P(("groups", "expert"), None, "tensor"),
            P("tensor", "expert"),
            P("groups", "expert"),
            P("expert"),
            P("groups", None),
            P("groups", None),
            P("expert", None, "tensor"),
            P("expert", None, "tensor"),
            P("expert", "tensor", None),
        ),
        out_specs=(P("groups", "expert"), P(("groups", "tensor"), "expert")),
        check_vma=False,
    )
```

time: 283 us -> 134 us (0.47)
  waiting for transfers between devices: 136 us -> 0 us
  Pallas kernels: 0 us -> 124 us
  starting transfers between devices: 67.9 us -> 0 us
  blocking collectives: 50.9 us -> 0 us
  other arithmetic: 7.48 us -> 0 us
  matrix products: 6.03 us -> 0 us
  local copies, waits for them, and re-layouts: 12.4 us -> 8.47 us
    all_to_all x5 -> x0, waiting for transfers between devices: 136 us -> none  [the longest x1 55.3 us: shards(): lax.all_to_all(ordered, 'expert', split_axis=0, concat_axis=1, tiled=True)]
    pallas_call x0 -> x1, Pallas kernels: none -> 124 us  [shards(): pl.pallas_call(functools.partial(kernel, ne, nt), out_shape=(jax.ShapeDty...]
    all_to_all x5 -> x0, starting transfers between devices: 67.9 us -> none  [the longest x1 45.2 us: shards(): lax.all_to_all(ordered, 'expert', split_axis=0, concat_axis=1, tiled=True)]
    all_to_all x2 -> x0, blocking collectives: 50.9 us -> none  [summed_on_arrival(): pieces = lax.all_to_all(cut_along(array, dim, size), axis, 0, 0, tiled=True)]
    unnamed x22 -> x28, local copies, waits for them, and re-layouts: 0.09 us -> 8.47 us
    gather x3 -> x0, local copies, waits for them, and re-layouts: 6.68 us -> none  [the longest x1 2.67 us: shards(): ordered = jnp.take(kv_prefill, slot_of, axis=0)]
    dot_general x6 -> x0, matrix products: 6.03 us -> none  [the longest x1 3.48 us: shards(): produced = jnp.dot(activated, down_slab, preferred_element_type=jnp.float32)]
    broadcast_in_dim x4 -> x0, local copies, waits for them, and re-layouts: 3.02 us -> none  [the longest x3 2.03 us: copy_for_each(): copies = jnp.broadcast_to(array, (lax.axis_size(axis), *array.shape))]
  transfers between devices with their start and end apart: 5 -> 0, of which waited for: 5 -> 0; matrix products, arithmetic and copies ran while one was open for 1% -> 0% of each run, Pallas kernels for 0% -> 0%
where the time goes in v1:
time: 134 us; the launch traced here: 133 us
  Pallas kernels  124 us (93%)
  local copies, waits for them, and re-layouts  8.47 us (6%)
    pallas_call x1, Pallas kernels, shards(): pl.pallas_call(functools.partial(kernel, ne, nt), out_shape=(jax.ShapeDty...  124 us
    unnamed x28, local copies, waits for them, and re-layouts  8.47 us

profile of v1, /device:TPU:65, one launch (start us, length us, event | category | flops | bytes accessed | tf_op | source)
XLA Modules:
  0.0 133.3 jit_solution(10204617758944999940)
XLA Ops:
  0.6 0.0 copy-start.12
  0.6 0.0 copy-start.9
  0.7 0.0 copy-start.11
  0.7 0.0 copy-start.6
  0.7 0.0 copy-start.7
  0.7 0.0 copy-start.8
  0.7 0.0 copy-start.10
  0.7 0.6 copy-done.12
  1.3 0.0 copy-done.9
  1.3 0.0 copy-done.11
  1.3 0.0 copy-done.6
  1.4 0.0 copy-done.7
  1.4 0.0 copy-done.8
  1.4 0.0 copy-done.10
  1.4 0.0 copy-start
  1.4 1.2 copy-done
  2.6 0.0 copy-start.1
  2.6 1.2 copy-done.1
  3.8 0.0 copy-start.2
  3.9 1.2 copy-done.2
  5.1 0.0 copy-start.3
  5.1 1.2 copy-done.3
  6.3 0.0 copy-start.4
  6.3 0.9 copy-done.4
  7.2 0.0 copy-start.5
  7.2 0.8 copy-done.5
  8.0 124.1 %shard_map.140 = (bf16[128,128]{1,0:T(8,128)(2,1)S(1)}, bf16[16,128]{1,0:T(8,128)(2,1)S(1)}) custom-call(s32[128]{0:T(128)S(1)} %copy-done.10, s32[1,128]{1,0:T(1,128)S(1)} %bitcast.14, s32[2,128]{1,0:T(2,128)S(1)} %bitcast.12, f32[2,128]{1,0:T(2,128)S(1)} %bitcast.13, bf16[4,512]{1,0:T(4,128)(2,1)S(1)} %copy-done.6, bf16[4,2,128]{2,1,0:T(2,128)(2,1)S(1)} %copy-done.7, ...), custom_call_target="tpu_custom_call" | custom-call | tf_op jit(solution)/shard_map/pallas_call | solution.py:557
  132.1 0.6 copy.17
  132.7 0.6 copy.18
Async XLA Ops:
  0.6 0.7 copy-start.12
  0.6 0.7 copy-start.9
  0.7 0.7 copy-start.11
  0.7 0.7 copy-start.6
  0.7 0.7 copy-start.7
  0.7 0.7 copy-start.8
  0.7 0.7 copy-start.10
  1.4 1.2 copy-start
  2.6 1.2 copy-start.1
  3.8 1.2 copy-start.2
  5.1 1.2 copy-start.3
  6.3 0.9 copy-start.4
  7.2 0.8 copy-start.5
